TPU v7x, 32 devices: a whole 2x2x4 slice. The times are simulated.
32 devices in a mesh: band: 4 (over y, x), grid: 8 (over z, core).
Axes of the slice: x: 2, y: 2, z: 4, core: 2. Of those that a mesh axis runs over, the one named last changes fastest.
Arguments:
- wavefunctions: bfloat16 [1024, 131072], P('band', 'grid'), may hold values from -6 to 6
- projectors: bfloat16 [512, 8, 13, 256], P('grid'), may hold values from -0.0068359375 to 0.0068359375
- slot_atom: int32 [512, 8], P('grid'), may hold values from -1 to 255, as said below
- occupations: float32 [1024], P('band'), may hold values from 0.02 to 2
Outputs:
- density: float32 [256, 13, 13], P('grid')
Inputs may be any that keep to these rules, and one draw needn't show every extreme that they name: `slot_atom`: -1 marks an empty slot. Any other entry is an atom a whose owning domain a // 32 lies within 3 domains, counted around the closed cycle of 8 domains, of the domain of the block, block index // 64. In every domain some block has all 8 slots filled.
All inputs are finite; a program needn't handle non-finite values.
Results may differ from a plain program's by a relative error of at most 0.0003.
Values sent between devices are 32-bit elements; how exact they have to be, the bound alone decides.
A program may use at most 64 MiB of HBM per device.

v0:
```python
import jax
import jax.numpy as jnp
from jax import lax
from jax.sharding import PartitionSpec as P

REACH = 3
ATOMS_DEV = 32


def shifted(block, axis, distance):
    devices = range(lax.axis_size(axis))
    route = [((i - distance) % len(devices), i) for i in devices]
    return lax.ppermute(block, axis, route)


def body(wavefunctions, projectors, slot_atom, occupations):
    band_count = wavefunctions.shape[0]
    block_count, capacity, proj_count, block_len = projectors.shape
    domains = lax.axis_size("grid")
    domain = lax.axis_index("grid")
    window_len = 2 * REACH + 1
    row_len = proj_count * band_count
    grid_blocks = wavefunctions.reshape(band_count, block_count, block_len)
    stacked = projectors.reshape(block_count, capacity * proj_count, block_len)
    slot_terms = jnp.einsum(
        "ngb,gcb->gcn", grid_blocks, stacked, preferred_element_type=jnp.float32
    )
    slot_terms = slot_terms.reshape(block_count * capacity, row_len)
    slot_ids = slot_atom.reshape(-1)
    owner = jnp.floor_divide(slot_ids, ATOMS_DEV)
    offset = jnp.mod(owner - domain + REACH, domains)
    target = jnp.where(
        slot_ids >= 0, offset * ATOMS_DEV + jnp.mod(slot_ids, ATOMS_DEV), window_len * ATOMS_DEV
    )
    selector = (
        jnp.arange(window_len * ATOMS_DEV, dtype=jnp.int32)[:, None] == target[None, :]
    ).astype(jnp.float32)
    window = jnp.dot(
        selector, slot_terms, precision=lax.Precision.HIGHEST, preferred_element_type=jnp.float32
    )
    window = window.reshape(window_len, ATOMS_DEV, row_len)
    forward = window[2 * REACH]
    for hop in range(REACH, 0, -1):
        forward = shifted(forward, "grid", 1) + window[REACH + hop - 1]
    backward = window[0]
    for hop in range(REACH, 0, -1):
        addend = window[REACH - hop + 1] if hop > 1 else jnp.zeros_like(backward)
        backward = shifted(backward, "grid", -1) + addend
    owned = forward + backward
    owned = owned.reshape(ATOMS_DEV, proj_count, band_count)
    weighted = owned * occupations.reshape(1, 1, band_count)
    partial_sum = jnp.einsum("ain,ajn->aij", weighted, owned, precision=lax.Precision.HIGHEST)
    density = lax.psum(partial_sum, "band")
    return density


def solution(mesh):
    in_specs = (P("band", "grid"), P("grid", None, None, None), P("grid", None), P("band"))
    out_specs = P("grid", None, None)
    return jax.shard_map(body, mesh=mesh, in_specs=in_specs, out_specs=out_specs, check_vma=False)
```

profile of v0, /device:TPU:0, one launch (start us, length us, event | category | flops | bytes accessed | tf_op | source)
XLA Modules:
  0.0 87.4 jit_solution(6354588679132287062)
XLA Ops:
  0.0 2.8 %copy.8 = bf16[64,8,13,256]{3,0,2,1:T(8,128)(2,1)S(1)} copy(bf16[64,8,13,256]{3,1,2,0:T(8,128)(2,1)} %param.5) | data formatting | bytes 6815744 | tf_op args[1]
  2.8 9.4 %fusion = f32[64,104,256]{2,1,0:T(8,128)} fusion(bf16[32,64,8,256]{3,2,1,0:T(8,128)(2,1)} %bitcast.8, bf16[64,104,256]{2,0,1:T(8,128)(2,1)S(1)} %bitcast.7), kind=kOutput, calls=%fused_computation | convolution fusion | flops 872415232 | bytes 18612224 | tf_op jit(solution)/shard_map/ngb,gcb->gcn/dot_general | solution.py:25
  12.2 0.0 copy-start
  12.2 8.5 %reshape.103 = f32[512,3328]{1,0:T(8,128)} reshape(f32[64,104,256]{2,1,0:T(8,128)} %fusion) | data formatting | bytes 13631488 | tf_op jit(solution)/shard_map/reshape | solution.py:28
  20.7 0.0 copy-done
  20.7 0.1 copy.7
  20.7 0.1 reshape.100
  20.9 6.3 %fusion.6 = f32[224,3328]{1,0:T(8,128)S(1)} fusion(f32[512,3328]{1,0:T(8,128)} %reshape.103, s32[512]{0:T(512)S(1)} %fusion.15), kind=kOutput, calls=%fused_computation.7 | convolution fusion | flops 4580294656 | bytes 9799680 | tf_op jit(solution)/shard_map/dot_general | solution.py:38
  27.1 0.1 fusion.17
  27.2 0.5 collective-permute-start
  27.8 0.0 copy-start.1
  27.8 4.1 %collective-permute-start.3 = (f32[32,3328]{1,0:T(8,128)S(1)}, f32[32,3328]{1,0:T(8,128)S(1)}, u32[]{:S(2)}, u32[]{:S(2)}) collective-permute-start(f32[32,3328]{1,0:T(8,128)S(1)} %get-tuple-element.10), channel_id=1, source_target_pairs={{1,0},{2,1},{3,2},{4,3},{5,4},{6,5},{7,6},{0,7},{9,8},{10,9},{11,1... | collective-permute-start | bytes 1277960 | tf_op jit(solution)/shard_map/ppermute | solution.py:13
  31.9 7.7 %collective-permute-done = f32[32,3328]{1,0:T(8,128)S(1)} collective-permute-done((f32[32,3328]{1,0:T(8,128)S(1)}, f32[32,3328]{1,0:T(8,128)S(1)}, u32[]{:S(2)}, u32[]{:S(2)}) %collective-permute-start) | collective-permute-done | bytes 426016 | tf_op jit(solution)/shard_map/ppermute | solution.py:13
  39.6 0.4 collective-permute-done.3
  40.0 0.1 slice_add_fusion.4
  40.1 2.0 %collective-permute-start.1 = (f32[32,3328]{1,0:T(8,128)S(1)}, f32[32,3328]{1,0:T(8,128)S(1)}, u32[]{:S(2)}, u32[]{:S(2)}) collective-permute-start(f32[32,3328]{1,0:T(8,128)S(1)} %get-tuple-element.7), channel_id=1, source_target_pairs={{7,0},{0,1},{1,2},{2,3},{3,4},{4,5},{5,6},{6,7},{15,8},{8,9},{9,10... | collective-permute-start | bytes 1277960 | tf_op jit(solution)/shard_map/ppermute | solution.py:13
  42.1 1.8 %collective-permute-start.4 = (f32[32,3328]{1,0:T(8,128)S(1)}, f32[32,3328]{1,0:T(8,128)S(1)}, u32[]{:S(2)}, u32[]{:S(2)}) collective-permute-start(f32[32,3328]{1,0:T(8,128)S(1)} %get-tuple-element.8), channel_id=1, source_target_pairs={{1,0},{2,1},{3,2},{4,3},{5,4},{6,5},{7,6},{0,7},{9,8},{10,9},{11,1... | collective-permute-start | bytes 1277960 | tf_op jit(solution)/shard_map/ppermute | solution.py:13
  44.0 7.6 %collective-permute-done.1 = f32[32,3328]{1,0:T(8,128)S(1)} collective-permute-done((f32[32,3328]{1,0:T(8,128)S(1)}, f32[32,3328]{1,0:T(8,128)S(1)}, u32[]{:S(2)}, u32[]{:S(2)}) %collective-permute-start.1) | collective-permute-done | bytes 426016 | tf_op jit(solution)/shard_map/ppermute | solution.py:13
  51.5 0.2 collective-permute-done.4
  51.7 0.1 slice_add_fusion.3
  51.8 2.5 %collective-permute-start.2 = (f32[32,3328]{1,0:T(8,128)S(1)}, f32[32,3328]{1,0:T(8,128)S(1)}, u32[]{:S(2)}, u32[]{:S(2)}) collective-permute-start(f32[32,3328]{1,0:T(8,128)S(1)} %get-tuple-element.5), channel_id=1, source_target_pairs={{7,0},{0,1},{1,2},{2,3},{3,4},{4,5},{5,6},{6,7},{15,8},{8,9},{9,10... | collective-permute-start | bytes 1277960 | tf_op jit(solution)/shard_map/ppermute | solution.py:13
  54.2 1.4 %collective-permute-start.5 = (f32[32,3328]{1,0:T(8,128)S(1)}, f32[32,3328]{1,0:T(8,128)S(1)}, u32[]{:S(2)}, u32[]{:S(2)}) collective-permute-start(f32[32,3328]{1,0:T(8,128)S(1)} %get-tuple-element.6), channel_id=1, source_target_pairs={{1,0},{2,1},{3,2},{4,3},{5,4},{6,5},{7,6},{0,7},{9,8},{10,9},{11,1... | collective-permute-start | bytes 1277960 | tf_op jit(solution)/shard_map/ppermute | solution.py:13
  55.7 7.1 %collective-permute-done.2 = f32[32,3328]{1,0:T(8,128)S(1)} collective-permute-done((f32[32,3328]{1,0:T(8,128)S(1)}, f32[32,3328]{1,0:T(8,128)S(1)}, u32[]{:S(2)}, u32[]{:S(2)}) %collective-permute-start.2) | collective-permute-done | bytes 426016 | tf_op jit(solution)/shard_map/ppermute | solution.py:13
  62.8 1.0 %collective-permute-done.5 = f32[32,3328]{1,0:T(8,128)S(1)} collective-permute-done((f32[32,3328]{1,0:T(8,128)S(1)}, f32[32,3328]{1,0:T(8,128)S(1)}, u32[]{:S(2)}, u32[]{:S(2)}) %collective-permute-start.5) | collective-permute-done | bytes 426016 | tf_op jit(solution)/shard_map/ppermute | solution.py:13
  63.8 0.1 fusion.7
  63.9 0.1 reshape.104
  64.0 0.0 copy-done.1
  64.0 0.6 fusion.4
  64.7 21.9 %psum.7 = f32[32,13,13]{2,1,0:T(8,128)S(1)} all-reduce(f32[32,13,13]{2,1,0:T(8,128)S(1)} %fusion.4), channel_id=1, replica_groups=mesh['band'=4,'grid'=8] {'band'}, use_global_device_ids=true, to_apply=%region_0.1 | all-reduce | flops 5408 | bytes 43264 | tf_op jit(solution)/shard_map/psum | solution.py:53
  86.6 0.8 copy.11
  (1 shorter events, 0.0 us)
Async XLA Ops:
  12.2 8.5 %copy-start = (s32[64,8]{0,1:T(8,128)S(1)}, s32[64,8]{0,1:T(8,128)}, u32[]{:S(2)}) copy-start(s32[64,8]{0,1:T(8,128)} %param.6) | copy-start | bytes 6148
  27.2 12.3 %collective-permute-start = (f32[32,3328]{1,0:T(8,128)S(1)}, f32[32,3328]{1,0:T(8,128)S(1)}, u32[]{:S(2)}, u32[]{:S(2)}) collective-permute-start(f32[32,3328]{1,0:T(8,128)S(1)} %get-tuple-element.9), channel_id=1, source_target_pairs={{7,0},{0,1},{1,2},{2,3},{3,4},{4,5},{5,6},{6,7},{15,8},{8,9},{9,10... | collective-permute-start | bytes 1277960 | tf_op jit(solution)/shard_map/ppermute | solution.py:13
  27.8 36.3 %copy-start.1 = (f32[256]{0:T(256)S(1)}, f32[256]{0:T(256)}, u32[]{:S(2)}) copy-start(f32[256]{0:T(256)} %param.7) | copy-start | bytes 3076
  27.8 12.2 %collective-permute-start.3 = (f32[32,3328]{1,0:T(8,128)S(1)}, f32[32,3328]{1,0:T(8,128)S(1)}, u32[]{:S(2)}, u32[]{:S(2)}) collective-permute-start(f32[32,3328]{1,0:T(8,128)S(1)} %get-tuple-element.10), channel_id=1, source_target_pairs={{1,0},{2,1},{3,2},{4,3},{5,4},{6,5},{7,6},{0,7},{9,8},{10,9},{11,1... | collective-permute-start | bytes 1277960 | tf_op jit(solution)/shard_map/ppermute | solution.py:13
  40.1 11.5 %collective-permute-start.1 = (f32[32,3328]{1,0:T(8,128)S(1)}, f32[32,3328]{1,0:T(8,128)S(1)}, u32[]{:S(2)}, u32[]{:S(2)}) collective-permute-start(f32[32,3328]{1,0:T(8,128)S(1)} %get-tuple-element.7), channel_id=1, source_target_pairs={{7,0},{0,1},{1,2},{2,3},{3,4},{4,5},{5,6},{6,7},{15,8},{8,9},{9,10... | collective-permute-start | bytes 1277960 | tf_op jit(solution)/shard_map/ppermute | solution.py:13
  42.1 9.6 %collective-permute-start.4 = (f32[32,3328]{1,0:T(8,128)S(1)}, f32[32,3328]{1,0:T(8,128)S(1)}, u32[]{:S(2)}, u32[]{:S(2)}) collective-permute-start(f32[32,3328]{1,0:T(8,128)S(1)} %get-tuple-element.8), channel_id=1, source_target_pairs={{1,0},{2,1},{3,2},{4,3},{5,4},{6,5},{7,6},{0,7},{9,8},{10,9},{11,1... | collective-permute-start | bytes 1277960 | tf_op jit(solution)/shard_map/ppermute | solution.py:13
  51.8 11.0 %collective-permute-start.2 = (f32[32,3328]{1,0:T(8,128)S(1)}, f32[32,3328]{1,0:T(8,128)S(1)}, u32[]{:S(2)}, u32[]{:S(2)}) collective-permute-start(f32[32,3328]{1,0:T(8,128)S(1)} %get-tuple-element.5), channel_id=1, source_target_pairs={{7,0},{0,1},{1,2},{2,3},{3,4},{4,5},{5,6},{6,7},{15,8},{8,9},{9,10... | collective-permute-start | bytes 1277960 | tf_op jit(solution)/shard_map/ppermute | solution.py:13
  54.2 9.6 %collective-permute-start.5 = (f32[32,3328]{1,0:T(8,128)S(1)}, f32[32,3328]{1,0:T(8,128)S(1)}, u32[]{:S(2)}, u32[]{:S(2)}) collective-permute-start(f32[32,3328]{1,0:T(8,128)S(1)} %get-tuple-element.6), channel_id=1, source_target_pairs={{1,0},{2,1},{3,2},{4,3},{5,4},{6,5},{7,6},{0,7},{9,8},{10,9},{11,1... | collective-permute-start | bytes 1277960 | tf_op jit(solution)/shard_map/ppermute | solution.py:13
where the time goes:
time: 87.8 us; the launch traced here: 87.4 us
  waiting for transfers between devices  24 us (27%)
  blocking collectives  21.9 us (25%)
  matrix products  16.3 us (19%)
  local copies, waits for them, and re-layouts  12.4 us (14%)
  starting transfers between devices  12.4 us (14%)
    ppermute x6, waiting for transfers between devices, shifted(): return lax.ppermute(block, axis, route)  24 us
    psum x1, blocking collectives, body(): density = lax.psum(partial_sum, 'band')  21.9 us
    ppermute x6, starting transfers between devices, shifted(): return lax.ppermute(block, axis, route)  12.4 us
    dot_general x1, matrix products, body(): jnp.einsum('ngb,gcb->gcn', grid_blocks, stacked, preferred_element_type=j...  9.38 us
    reshape x1, local copies, waits for them, and re-layouts, body(): slot_terms = slot_terms.reshape(block_count * capacity, row_len)  8.49 us
    dot_general x1, matrix products, body(): jnp.dot(selector, slot_terms, precision=lax.Precision.HIGHEST, preferred_...  6.29 us
    unnamed x6, local copies, waits for them, and re-layouts  2.86 us
  transfers between devices with their start and end apart: 6, of which 6 were waited for; matrix products, arithmetic and copies ran while one was open for 0% of the time, Pallas kernels for 0%

commit v1 on v0

v1 whole, which is shorter than its diff:
```python
import functools

import jax
import jax.numpy as jnp
from jax import lax
from jax.experimental import pallas as pl
from jax.experimental.pallas import tpu as pltpu
from jax.sharding import PartitionSpec as P

REACH = 3
ATOMS_DEV = 32
ROWS = 8
LANES = 128
STRIDE = 16
SKEW = 2
STEP_BLOCKS = 8
MESH = pl.DeviceIdType.MESH
HIGHEST = lax.Precision.HIGHEST


def nt_dot(a, b, precision=None):
    return lax.dot_general(
        a, b, (((1,), (1,)), ((), ())), precision=precision, preferred_element_type=jnp.float32
    )


def local_kernel(ids_ref, waves_ref, pieces_ref, out_ref, slots, padded):
    step = pl.program_id(0)
    per_step, capacity, proj_count, block_len = pieces_ref.shape
    bands = waves_ref.shape[0]
    halves, _, targets, lanes = out_ref.shape
    height = padded.shape[2]

    @pl.when(step == 0)
    def _():
        padded[...] = jnp.zeros_like(padded)

    row = lax.broadcasted_iota(jnp.int32, (proj_count * capacity, capacity * height), 0)
    col = lax.broadcasted_iota(jnp.int32, (proj_count * capacity, capacity * height), 1)
    swap = (col == (row % capacity) * height + row // capacity).astype(jnp.bfloat16)
    for g in range(per_step):
        padded[g, :, :proj_count, :] = pieces_ref[g]
    for g in range(per_step):
        stacked = padded[g].reshape(capacity * height, block_len)
        ordered = jnp.dot(swap, stacked, preferred_element_type=jnp.float32).astype(jnp.bfloat16)
        terms = nt_dot(ordered, waves_ref[:, g * block_len:(g + 1) * block_len])
        start = pl.multiple_of((step * per_step + g) * capacity, capacity)
        for i in range(proj_count):
            slots[pl.ds(start, capacity), i * bands:(i + 1) * bands] = terms[i * capacity:(i + 1) * capacity]

    @pl.when(step == pl.num_programs(0) - 1)
    def _():
        slot_count = slots.shape[0]
        wanted = lax.broadcasted_iota(jnp.int32, (targets, slot_count), 0)
        pick = (wanted == ids_ref[...]).astype(jnp.bfloat16)
        for i in range(proj_count):
            full = slots[:, i * bands:(i + 1) * bands]
            high = full.astype(jnp.bfloat16)
            low = (full - high.astype(jnp.float32)).astype(jnp.bfloat16)
            total = jnp.dot(pick, high, preferred_element_type=jnp.float32)
            total += jnp.dot(pick, low, preferred_element_type=jnp.float32)
            for h in range(halves):
                out_ref[h, i] = total[:, h * lanes:(h + 1) * lanes]


def local_window(wavefunctions, projectors, slot_ids, targets):
    bands = wavefunctions.shape[0]
    blocks, capacity, proj_count, block_len = projectors.shape
    height = -(-proj_count // 16) * 16
    shape = (bands // LANES, proj_count, targets, LANES)
    return pl.pallas_call(
        local_kernel,
        grid=(blocks // STEP_BLOCKS,),
        in_specs=[
            pl.BlockSpec((1, blocks * capacity), lambda s: (0, 0)),
            pl.BlockSpec((bands, STEP_BLOCKS * block_len), lambda s: (0, s)),
            pl.BlockSpec((STEP_BLOCKS, capacity, proj_count, block_len), lambda s: (s, 0, 0, 0)),
        ],
        out_specs=pl.BlockSpec(shape, lambda s: (0, 0, 0, 0)),
        out_shape=jax.ShapeDtypeStruct(shape, jnp.float32),
        scratch_shapes=[
            pltpu.VMEM((blocks * capacity, proj_count * bands), jnp.float32),
            pltpu.VMEM((STEP_BLOCKS, capacity, height, block_len), jnp.bfloat16),
        ],
        compiler_params=pltpu.CompilerParams(vmem_limit_bytes=40 << 20),
    )(slot_ids.reshape(1, -1), wavefunctions, projectors)


def reduce_kernel(groups, band_size, win, occ, out_ref, pair_in, hop_in, summed, mine, peers, final, landed,
                  pair_send, pair_recv, hop_send, hop_recv, peer_send, peer_recv, last_send, last_recv):
    halves, proj_count, _, lanes = win.shape
    band = lax.axis_index("band")
    domain = lax.axis_index("grid")
    core = domain % 2
    chip = domain // 2
    chips = groups // 2
    turns = chips // 2
    subs = ATOMS_DEV // ROWS
    per_turn = subs * halves
    chunks = turns * per_turn
    top = (proj_count + 1) // 2 * ROWS
    rows = proj_count * ROWS

    barrier = pltpu.get_barrier_semaphore()
    partner = (band, chip * 2 + 1 - core)
    met = [partner]
    for r in range(1, chips):
        met.append((band, ((chip + r) % chips) * 2 + core))
    for r in range(1, band_size):
        met.append(((band + r) % band_size, domain))
    for other in met:
        pl.semaphore_signal(barrier, inc=1, device_id=other, device_id_type=MESH)

    def place(direction, k):
        block = k // halves
        turn = block // subs
        owner = turns - 1 - turn if direction == 0 else turns + turn
        return k % halves, pl.multiple_of(block * ROWS, ROWS), owner, block % subs

    def pair_copy(direction, k):
        half, at, owner, sub = place(direction, k)
        source = pl.multiple_of((owner * 2 + 1 - core) * ATOMS_DEV + sub * ROWS, ROWS)
        return pltpu.make_async_remote_copy(
            src_ref=win.at[half, :, pl.ds(source, ROWS), :],
            dst_ref=pair_in.at[direction, half, :, pl.ds(at, ROWS), :],
            send_sem=pair_send.at[direction, k], recv_sem=pair_recv.at[direction, k],
            device_id=partner, device_id_type=MESH,
        )

    def hop_copy(direction, k):
        half, at, _, _ = place(direction, k)
        following = chip - 1 if direction == 0 else chip + 1
        return pltpu.make_async_remote_copy(
            src_ref=summed.at[direction, half, :, pl.ds(at, ROWS), :],
            dst_ref=hop_in.at[direction, half, :, pl.ds(at, ROWS), :],
            send_sem=hop_send.at[direction, k], recv_sem=hop_recv.at[direction, k],
            device_id=(band, following * 2 + core), device_id_type=MESH,
        )

    def peer_copy(turn, r):
        return pltpu.make_async_remote_copy(
            src_ref=mine.at[turn], dst_ref=peers.at[turn, r - 1],
            send_sem=peer_send.at[turn, r - 1], recv_sem=peer_recv.at[turn, r - 1],
            device_id=((band + r) % band_size, domain), device_id_type=MESH,
        )

    def last_copy(direction, turn):
        owner = turns - 1 - turn if direction == 0 else turns + turn
        return pltpu.make_async_remote_copy(
            src_ref=final.at[turn], dst_ref=landed,
            send_sem=last_send.at[turn], recv_sem=last_recv,
            device_id=(band, owner * 2 + core), device_id_type=MESH,
        )

    def summed_peers(turn):
        total = mine[turn]
        for r in range(1, band_size):
            peer_copy(turn, r).wait_recv()
            total = total + peers[turn, r - 1]
        return total

    mine[...] = jnp.zeros_like(mine)
    pl.semaphore_wait(barrier, len(met))

    @pl.loop(0, chunks)
    def _(k):
        for direction in range(2):
            pair_copy(direction, k).start()

    def density(direction, k):
        half, at, _, sub = place(direction, k)
        x = summed[direction, half, :, pl.ds(at, ROWS), :].reshape(rows, lanes)
        gram = nt_dot(x * occ[half], x, HIGHEST)
        r = lax.broadcasted_iota(jnp.int32, (rows, rows), 0)
        c = lax.broadcasted_iota(jnp.int32, (rows, rows), 1)
        gram = jnp.where(r % ROWS == c % ROWS, gram, 0.0)
        j = lax.broadcasted_iota(jnp.int32, (rows, LANES), 0) // ROWS
        lane = lax.broadcasted_iota(jnp.int32, (rows, LANES), 1)
        upper = (lane == sub * STRIDE + j).astype(jnp.float32)
        lower = (lane == (subs + sub) * STRIDE + j).astype(jnp.float32)
        turn = k // per_turn
        mine[turn, :, :] += jnp.dot(gram[:top], upper, precision=HIGHEST, preferred_element_type=jnp.float32)
        mine[turn, :rows - top, :] += jnp.dot(gram[top:], lower, precision=HIGHEST, preferred_element_type=jnp.float32)
        for turn in range(turns):
            @pl.when(k == (turn + 1) * per_turn - 1)
            def _():
                for r in range(1, band_size):
                    peer_copy(turn, r).start()
        for turn in range(turns - 1):
            @pl.when(k == (turn + 1) * per_turn - 1 + per_turn // 2)
            def _():
                final[turn] = summed_peers(turn)
                last_copy(direction, turn).start()

    def process(direction, k, hops):
        half, at, owner, sub = place(direction, k)
        source = pl.multiple_of((owner * 2 + core) * ATOMS_DEV + sub * ROWS, ROWS)
        here = (direction, half, slice(None), pl.ds(at, ROWS), slice(None))
        pair_copy(direction, k).wait_recv()
        summed[here] = win[half, :, pl.ds(source, ROWS), :] + pair_in[here]

        @pl.when(hops > 0)
        def _():
            hop_copy(direction, k).wait_recv()
            summed[here] = summed[here] + hop_in[here]

        @pl.when(hops < chips - 1)
        def _():
            hop_copy(direction, k).start()

        @pl.when(hops == chips - 1)
        def _():
            density(direction, k)

    @pl.loop(0, chunks + SKEW * (chips - 1))
    def _(t):
        for direction in range(2):
            hops = chips - 1 - chip if direction == 0 else chip
            k = t - SKEW * hops

            @pl.when((k >= 0) & (k < chunks))
            def _():
                process(direction, k, hops)

    edge = (chip == 0) | (chip == chips - 1)

    @pl.when(edge)
    def _():
        out_ref[...] = summed_peers(turns - 1)
        for turn in range(turns):
            for r in range(1, band_size):
                peer_copy(turn, r).wait_send()
        for turn in range(turns - 1):
            last_copy(0, turn).wait_send()

    @pl.when(jnp.logical_not(edge))
    def _():
        last_copy(0, 0).wait_recv()
        out_ref[...] = landed[...]

    @pl.loop(0, chunks)
    def _(k):
        for direction in range(2):
            hops = chips - 1 - chip if direction == 0 else chip
            pair_copy(direction, k).wait_send()

            @pl.when(hops < chips - 1)
            def _():
                hop_copy(direction, k).wait_send()


def reduce_density(window, occupations, groups, band_size):
    halves, proj_count, _, lanes = window.shape
    turns = groups // 4
    chunks = turns * ATOMS_DEV // ROWS * halves
    top = (proj_count + 1) // 2 * ROWS
    handled = (2, halves, proj_count, turns * ATOMS_DEV, lanes)
    vmem = pl.BlockSpec(memory_space=pltpu.VMEM)
    dma = pltpu.SemaphoreType.DMA
    packed = pl.pallas_call(
        functools.partial(reduce_kernel, groups, band_size),
        in_specs=[vmem, vmem],
        out_specs=vmem,
        out_shape=jax.ShapeDtypeStruct((top, LANES), jnp.float32),
        scratch_shapes=[
            pltpu.VMEM(handled, jnp.float32),
            pltpu.VMEM(handled, jnp.float32),
            pltpu.VMEM(handled, jnp.float32),
            pltpu.VMEM((turns, top, LANES), jnp.float32),
            pltpu.VMEM((turns, band_size - 1, top, LANES), jnp.float32),
            pltpu.VMEM((turns, top, LANES), jnp.float32),
            pltpu.VMEM((top, LANES), jnp.float32),
            dma((2, chunks)), dma((2, chunks)), dma((2, chunks)), dma((2, chunks)),
            dma((turns, band_size - 1)), dma((turns, band_size - 1)), dma((turns,)), dma,
        ],
        compiler_params=pltpu.CompilerParams(
            collective_id=0, has_side_effects=True, vmem_limit_bytes=40 << 20
        ),
    )(window, occupations.reshape(halves, 1, lanes))
    subs = ATOMS_DEV // ROWS
    packed = packed.reshape(top // ROWS, ROWS, 2, subs, STRIDE).transpose(3, 1, 2, 0, 4)
    packed = packed.reshape(ATOMS_DEV, 2 * top // ROWS, STRIDE)
    return packed[:, :proj_count, :proj_count]


def shifted(block, axis, distance):
    devices = range(lax.axis_size(axis))
    route = [((i - distance) % len(devices), i) for i in devices]
    return lax.ppermute(block, axis, route)


def ring_density(wavefunctions, projectors, slot_ids, occupations):
    domains = lax.axis_size("grid")
    domain = lax.axis_index("grid")
    window_len = 2 * REACH + 1
    owner = jnp.floor_divide(slot_ids, ATOMS_DEV)
    offset = jnp.mod(owner - domain + REACH, domains)
    target = jnp.where(slot_ids >= 0, offset * ATOMS_DEV + jnp.mod(slot_ids, ATOMS_DEV), -1)
    window = local_window(wavefunctions, projectors, target, window_len * ATOMS_DEV)
    halves, proj_count, _, lanes = window.shape
    window = window.reshape(halves, proj_count, window_len, ATOMS_DEV, lanes)
    part = lambda at: window[:, :, at]
    forward = part(2 * REACH)
    for hop in range(REACH, 0, -1):
        forward = shifted(forward, "grid", 1) + part(REACH + hop - 1)
    backward = part(0)
    for hop in range(REACH, 0, -1):
        backward = shifted(backward, "grid", -1)
        if hop > 1:
            backward = backward + part(REACH - hop + 1)
    owned = forward + backward
    weighted = owned * occupations.reshape(halves, 1, 1, lanes)
    partial_sum = jnp.einsum("hian,hjan->aij", weighted, owned, precision=HIGHEST)
    return lax.psum(partial_sum, "band")


def body(wavefunctions, projectors, slot_atom, occupations):
    domains = lax.axis_size("grid")
    slot_ids = slot_atom.reshape(-1)
    if domains <= 2 * REACH + 2 and domains % 4 == 0:
        window = local_window(wavefunctions, projectors, slot_ids, domains * ATOMS_DEV)
        return reduce_density(window, occupations, domains, lax.axis_size("band"))
    return ring_density(wavefunctions, projectors, slot_ids, occupations)


def solution(mesh):
    in_specs = (P("band", "grid"), P("grid", None, None, None), P("grid", None), P("band"))
    out_specs = P("grid", None, None)
    return jax.shard_map(body, mesh=mesh, in_specs=in_specs, out_specs=out_specs, check_vma=False)
```

time: 87.8 us -> 61.6 us (0.70)
  Pallas kernels: 0 us -> 56.1 us
  waiting for transfers between devices: 24 us -> 0 us
  blocking collectives: 21.9 us -> 0 us
  matrix products: 16.3 us -> 0 us
  starting transfers between devices: 12.4 us -> 0 us
  local copies, waits for them, and re-layouts: 12.4 us -> 5.16 us
    pallas_call x0 -> x2, Pallas kernels: none -> 56.1 us  [the longest x1 44.9 us: reduce_density(): pl.pallas_call(functools.partial(reduce_kernel, groups, band_size), in_sp...]
    ppermute x6 -> x0, waiting for transfers between devices: 24 us -> none  [shifted(): return lax.ppermute(block, axis, route)]
    psum x1 -> x0, blocking collectives: 21.9 us -> none  [body(): density = lax.psum(partial_sum, 'band')]
    dot_general x3 -> x0, matrix products: 16.3 us -> none  [the longest x1 9.38 us: body(): jnp.einsum('ngb,gcb->gcn', grid_blocks, stacked, preferred_element_type=j...]
    ppermute x6 -> x0, starting transfers between devices: 12.4 us -> none  [shifted(): return lax.ppermute(block, axis, route)]
    reshape x3 -> x2, local copies, waits for them, and re-layouts: 8.72 us -> 0.24 us  [reduce_density(): packed.reshape(top // ROWS, ROWS, 2, subs, STRIDE).transpose(3, 1, 2, 0, 4)]
    unnamed x6 -> x4, local copies, waits for them, and re-layouts: 2.86 us -> 4.03 us
  transfers between devices with their start and end apart: 6 -> 0, of which waited for: 6 -> 0; matrix products, arithmetic and copies ran while one was open for 0% -> 0% of each run, Pallas kernels for 0% -> 0%
where the time goes in v1:
time: 61.6 us; the launch traced here: 61.3 us
  Pallas kernels  56.1 us (91%)
  local copies, waits for them, and re-layouts  5.16 us (8%)
    pallas_call x1, Pallas kernels, reduce_density(): pl.pallas_call(functools.partial(reduce_kernel, groups, band_size), in_sp...  44.9 us
    pallas_call x1, Pallas kernels, local_window(): pl.pallas_call(local_kernel, grid=(blocks // STEP_BLOCKS,), in_specs=[pl....  11.2 us
    unnamed x4, local copies, waits for them, and re-layouts  4.03 us

profile of v1, /device:TPU:0, one launch (start us, length us, event | category | flops | bytes accessed | tf_op | source)
XLA Modules:
  0.0 61.3 jit_solution(1983585589910980282)
XLA Ops:
  0.0 0.8 %copy.8 = s32[64,8]{1,0:T(8,128)S(1)} copy(s32[64,8]{0,1:T(8,128)} %param.6) | data formatting | bytes 4096 | tf_op args[2]
  0.8 0.1 reshape_reshape.3.ids_ref
  0.9 3.2 %copy.9.pieces_ref = bf16[64,8,13,256]{3,2,1,0:T(8,128)(2,1)S(1)} copy(bf16[64,8,13,256]{3,1,2,0:T(8,128)(2,1)} %param.5) | data formatting | bytes 6815744 | tf_op args[1]
  4.1 0.0 copy-start
  4.1 11.2 %shard_map.46.win = f32[2,13,256,128]{3,2,1,0:T(8,128)S(1)} custom-call(s32[1,512]{1,0:T(1,128)S(1)} %reshape_reshape.3.ids_ref, bf16[256,16384]{1,0:T(8,128)(2,1)} %waves_ref.1, bf16[64,8,13,256]{3,2,1,0:T(8,128)(2,1)S(1)} %copy.9.pieces_ref), custom_call_target="tpu_custom_call" | custom-call | tf_op jit(solution)/shard_map/pallas_call | solution.py:71
  15.3 0.0 copy-done
  15.3 44.9 %shard_map.47 = f32[56,128]{1,0:T(8,128)S(1)} custom-call(f32[2,13,256,128]{3,2,1,0:T(8,128)S(1)} %shard_map.46.win, f32[2,1,128]{2,1,0:T(1,128)S(1)} %bitcast.4), custom_call_target="tpu_custom_call" | custom-call | tf_op jit(solution)/shard_map/pallas_call | solution.py:260
  60.2 0.2 reshape.10
  60.5 0.8 %copy.11 = f32[32,13,13]{0,2,1:T(8,128)} copy(f32[32,13,13]{2,0,1:T(8,128)S(1)} %slice.4) | data formatting | bytes 43264 | tf_op jit(solution)/shard_map/slice | solution.py:283
  (2 shorter events, 0.1 us)
Async XLA Ops:
  4.1 11.2 %copy-start = (f32[256]{0:T(256)S(1)}, f32[256]{0:T(256)}, u32[]{:S(2)}) copy-start(f32[256]{0:T(256)} %param.7) | copy-start | bytes 3076

commit v2 on v1

--- a/solution.py
+++ b/solution.py
@@ -12,7 +12,7 @@
 ROWS = 8
 LANES = 128
 STRIDE = 16
-SKEW = 2
+SKEW = 3
 STEP_BLOCKS = 8
 MESH = pl.DeviceIdType.MESH
 HIGHEST = lax.Precision.HIGHEST
@@ -24,26 +24,19 @@
     )
 
 
-def local_kernel(ids_ref, waves_ref, pieces_ref, out_ref, slots, padded):
+def split(full):
+    high = full.astype(jnp.bfloat16)
+    return high, (full - high.astype(jnp.float32)).astype(jnp.bfloat16)
+
+
+def local_kernel(ids_ref, waves_ref, pieces_ref, out_ref, slots):
     step = pl.program_id(0)
-    per_step, capacity, proj_count, block_len = pieces_ref.shape
+    per_step, proj_count, capacity, block_len = pieces_ref.shape
     bands = waves_ref.shape[0]
     halves, _, targets, lanes = out_ref.shape
-    height = padded.shape[2]
-
-    @pl.when(step == 0)
-    def _():
-        padded[...] = jnp.zeros_like(padded)
-
-    row = lax.broadcasted_iota(jnp.int32, (proj_count * capacity, capacity * height), 0)
-    col = lax.broadcasted_iota(jnp.int32, (proj_count * capacity, capacity * height), 1)
-    swap = (col == (row % capacity) * height + row // capacity).astype(jnp.bfloat16)
     for g in range(per_step):
-        padded[g, :, :proj_count, :] = pieces_ref[g]
-    for g in range(per_step):
-        stacked = padded[g].reshape(capacity * height, block_len)
-        ordered = jnp.dot(swap, stacked, preferred_element_type=jnp.float32).astype(jnp.bfloat16)
-        terms = nt_dot(ordered, waves_ref[:, g * block_len:(g + 1) * block_len])
+        stacked = pieces_ref[g].reshape(proj_count * capacity, block_len)
+        terms = nt_dot(stacked, waves_ref[:, g * block_len:(g + 1) * block_len])
         start = pl.multiple_of((step * per_step + g) * capacity, capacity)
         for i in range(proj_count):
             slots[pl.ds(start, capacity), i * bands:(i + 1) * bands] = terms[i * capacity:(i + 1) * capacity]
@@ -55,8 +48,7 @@
         pick = (wanted == ids_ref[...]).astype(jnp.bfloat16)
         for i in range(proj_count):
             full = slots[:, i * bands:(i + 1) * bands]
-            high = full.astype(jnp.bfloat16)
-            low = (full - high.astype(jnp.float32)).astype(jnp.bfloat16)
+            high, low = split(full)
             total = jnp.dot(pick, high, preferred_element_type=jnp.float32)
             total += jnp.dot(pick, low, preferred_element_type=jnp.float32)
             for h in range(halves):
@@ -66,7 +58,6 @@
 def local_window(wavefunctions, projectors, slot_ids, targets):
     bands = wavefunctions.shape[0]
     blocks, capacity, proj_count, block_len = projectors.shape
-    height = -(-proj_count // 16) * 16
     shape = (bands // LANES, proj_count, targets, LANES)
     return pl.pallas_call(
         local_kernel,
@@ -74,16 +65,15 @@
         in_specs=[
             pl.BlockSpec((1, blocks * capacity), lambda s: (0, 0)),
             pl.BlockSpec((bands, STEP_BLOCKS * block_len), lambda s: (0, s)),
-            pl.BlockSpec((STEP_BLOCKS, capacity, proj_count, block_len), lambda s: (s, 0, 0, 0)),
+            pl.BlockSpec((STEP_BLOCKS, proj_count, capacity, block_len), lambda s: (s, 0, 0, 0)),
         ],
         out_specs=pl.BlockSpec(shape, lambda s: (0, 0, 0, 0)),
         out_shape=jax.ShapeDtypeStruct(shape, jnp.float32),
         scratch_shapes=[
             pltpu.VMEM((blocks * capacity, proj_count * bands), jnp.float32),
-            pltpu.VMEM((STEP_BLOCKS, capacity, height, block_len), jnp.bfloat16),
         ],
-        compiler_params=pltpu.CompilerParams(vmem_limit_bytes=40 << 20),
-    )(slot_ids.reshape(1, -1), wavefunctions, projectors)
+        compiler_params=pltpu.CompilerParams(vmem_limit_bytes=60 << 20),
+    )(slot_ids.reshape(1, -1), wavefunctions, projectors.transpose(0, 2, 1, 3))
 
 
 def reduce_kernel(groups, band_size, win, occ, out_ref, pair_in, hop_in, summed, mine, peers, final, landed,
@@ -168,19 +158,27 @@
             pair_copy(direction, k).start()
 
     def density(direction, k):
-        half, at, _, sub = place(direction, k)
-        x = summed[direction, half, :, pl.ds(at, ROWS), :].reshape(rows, lanes)
-        gram = nt_dot(x * occ[half], x, HIGHEST)
-        r = lax.broadcasted_iota(jnp.int32, (rows, rows), 0)
-        c = lax.broadcasted_iota(jnp.int32, (rows, rows), 1)
-        gram = jnp.where(r % ROWS == c % ROWS, gram, 0.0)
-        j = lax.broadcasted_iota(jnp.int32, (rows, LANES), 0) // ROWS
-        lane = lax.broadcasted_iota(jnp.int32, (rows, LANES), 1)
-        upper = (lane == sub * STRIDE + j).astype(jnp.float32)
-        lower = (lane == (subs + sub) * STRIDE + j).astype(jnp.float32)
-        turn = k // per_turn
-        mine[turn, :, :] += jnp.dot(gram[:top], upper, precision=HIGHEST, preferred_element_type=jnp.float32)
-        mine[turn, :rows - top, :] += jnp.dot(gram[top:], lower, precision=HIGHEST, preferred_element_type=jnp.float32)
+        _, at, _, sub = place(direction, k)
+
+        @pl.when(k % halves == halves - 1)
+        def _():
+            x = [summed[direction, h, :, pl.ds(at, ROWS), :].reshape(rows, lanes) for h in range(halves)]
+            left = split(jnp.concatenate([x[h] * occ[h] for h in range(halves)], axis=1))
+            right = split(jnp.concatenate(x, axis=1))
+            gram = nt_dot(left[0], right[0]) + nt_dot(left[0], right[1]) + nt_dot(left[1], right[0])
+            r = lax.broadcasted_iota(jnp.int32, (rows, rows), 0)
+            c = lax.broadcasted_iota(jnp.int32, (rows, rows), 1)
+            gram = split(jnp.where(r % ROWS == c % ROWS, gram, 0.0))
+            j = lax.broadcasted_iota(jnp.int32, (rows, LANES), 0) // ROWS
+            lane = lax.broadcasted_iota(jnp.int32, (rows, LANES), 1)
+            gather = (lane % (subs * STRIDE) == sub * STRIDE + j).astype(jnp.bfloat16)
+            packed = jnp.dot(gram[0], gather, preferred_element_type=jnp.float32)
+            packed += jnp.dot(gram[1], gather, preferred_element_type=jnp.float32)
+            turn = k // per_turn
+            low_lane = lane < subs * STRIDE
+            mine[turn, :, :] += jnp.where(low_lane[:top], packed[:top], 0.0)
+            mine[turn, :rows - top, :] += jnp.where(low_lane[top:], 0.0, packed[top:])
+
         for turn in range(turns):
             @pl.when(k == (turn + 1) * per_turn - 1)
             def _():

time: 61.6 us -> 55.2 us (0.90)
  Pallas kernels: 56.1 us -> 50.4 us
  local copies, waits for them, and re-layouts: 5.16 us -> 4.45 us
    pallas_call x1, Pallas kernels: 44.9 us -> 38.7 us  [reduce_density(): pl.pallas_call(functools.partial(reduce_kernel, groups, band_size), in_sp...]
    unnamed x4 -> x5, local copies, waits for them, and re-layouts: 4.03 us -> 2.74 us
where the time goes in v2:
time: 55.2 us; the launch traced here: 54.9 us
  Pallas kernels  50.4 us (91%)
  local copies, waits for them, and re-layouts  4.45 us (8%)
    pallas_call x1, Pallas kernels, reduce_density(): pl.pallas_call(functools.partial(reduce_kernel, groups, band_size), in_sp...  38.7 us
    pallas_call x1, Pallas kernels, local_window(): pl.pallas_call(local_kernel, grid=(blocks // STEP_BLOCKS,), in_specs=[pl....  11.7 us
    unnamed x5, local copies, waits for them, and re-layouts  2.74 us

profile of v2, /device:TPU:0, one launch (start us, length us, event | category | flops | bytes accessed | tf_op | source)
XLA Modules:
  0.0 54.9 jit_solution(6400847571819639988)
XLA Ops:
  0.0 0.8 %copy.7 = s32[64,8]{1,0:T(8,128)S(1)} copy(s32[64,8]{0,1:T(8,128)} %param.6) | data formatting | bytes 4096 | tf_op args[2]
  0.8 0.7 %reshape_reshape.3.ids_ref = s32[1,512]{1,0:T(1,128)} reshape(s32[64,8]{1,0:T(8,128)S(1)} %copy.7) | data formatting | bytes 4096 | tf_op jit(solution)/shard_map/reshape;reshape | solution.py:76
  1.4 0.0 copy-start.1
  1.4 11.7 %shard_map.46.win = f32[2,13,256,128]{3,2,1,0:T(8,128)} custom-call(s32[1,512]{1,0:T(1,128)} %reshape_reshape.3.ids_ref, bf16[256,16384]{1,0:T(8,128)(2,1)} %waves_ref.1, bf16[64,13,8,256]{3,2,1,0:T(8,128)(2,1)} %bitcast.6), custom_call_target="tpu_custom_call" | custom-call | tf_op jit(solution)/shard_map/pallas_call | solution.py:62
  13.2 0.0 copy-done.1
  13.2 0.0 copy-start
  13.2 2.0 %copy-done = f32[2,13,256,128]{3,2,1,0:T(8,128)S(1)} copy-done((f32[2,13,256,128]{3,2,1,0:T(8,128)S(1)}, f32[2,13,256,128]{3,2,1,0:T(8,128)}, u32[]{:S(2)}) %copy-start) | copy-done | bytes 3407896
  15.2 38.7 %shard_map.47 = f32[56,128]{1,0:T(8,128)S(1)} custom-call(f32[2,13,256,128]{3,2,1,0:T(8,128)S(1)} %copy-done, f32[2,1,128]{2,1,0:T(1,128)S(1)} %bitcast.5), custom_call_target="tpu_custom_call" | custom-call | tf_op jit(solution)/shard_map/pallas_call | solution.py:258
  53.8 0.2 reshape.10
  54.1 0.8 %copy.9 = f32[32,13,13]{0,2,1:T(8,128)} copy(f32[32,13,13]{2,0,1:T(8,128)S(1)} %slice.4) | data formatting | bytes 43264 | tf_op jit(solution)/shard_map/slice | solution.py:281
  (2 shorter events, 0.1 us)
Async XLA Ops:
  1.4 11.7 %copy-start.1 = (f32[256]{0:T(256)S(1)}, f32[256]{0:T(256)}, u32[]{:S(2)}) copy-start(f32[256]{0:T(256)} %param.7) | copy-start | bytes 3076
  13.2 2.0 %copy-start = (f32[2,13,256,128]{3,2,1,0:T(8,128)S(1)}, f32[2,13,256,128]{3,2,1,0:T(8,128)}, u32[]{:S(2)}) copy-start(f32[2,13,256,128]{3,2,1,0:T(8,128)} %shard_map.46.win) | copy-start | bytes 10223620
